TPU v7x, 32 devices: a whole 2x2x4 slice. The times are simulated.
32 devices in a mesh: tm: 16 (over z, y, x), batch: 2 (over core).
Axes of the slice: x: 2, y: 2, z: 4, core: 2. Of those that a mesh axis runs over, the one named last changes fastest.
Arguments:
- state_map: float32 [512, 256, 256], P(('batch', 'tm')), parts along dimension 0, may hold values from -0.375 to 0.375
- input_map: float32 [512, 64, 256], P(('batch', 'tm')), parts along dimension 0, may hold values from -0.375 to 0.375
- closed_loop: float32 [512, 256, 256], P(('batch', 'tm')), parts along dimension 0, may hold values from -1.001 to 1.001
- feedback: float32 [512, 64, 256], P(('batch', 'tm')), parts along dimension 0, may hold values from -0.375 to 0.375
- value_matrix: float32 [512, 256, 256], P(('batch', 'tm')), parts along dimension 0, may hold values from -0.046875 to 1.5, as said below
- gain_inverse: float32 [512, 64, 64], P(('batch', 'tm')), parts along dimension 0, may hold values from -0.0105 to 0.2, as said below
- input_weight: float32 [128, 64], P('batch'), parts along dimension 0, may hold values from -0.36 to 6, as said below
- state_weight: float32 [512, 256], P(('batch', 'tm')), parts along dimension 0, may hold values from 0.1 to 3
- state_linear: float32 [512, 256], P(('batch', 'tm')), parts along dimension 0, may hold values from -0.18 to 0.18
- input_linear: float32 [512, 64], P(('batch', 'tm')), parts along dimension 0, may hold values from -0.18 to 0.18
- offset: float32 [512, 256], P(('batch', 'tm')), parts along dimension 0, may hold values from -0.18 to 0.18
- upper_bound: float32 [512, 64], P(('batch', 'tm')), parts along dimension 0, may hold values from 0.1 to 0.3
- states: float32 [512, 256], P(('batch', 'tm')), parts along dimension 0, may hold values from -0.18 to 0.18
- inputs: float32 [512, 64], P(('batch', 'tm')), parts along dimension 0, may hold values from -0.18 to 0.18
- multipliers: float32 [512, 256], P(('batch', 'tm')), parts along dimension 0, may hold values from -0.18 to 0.18
- bound_mult: float32 [512, 64], P(('batch', 'tm')), parts along dimension 0, may hold values from 0 to 0.06
- active: int32 [512, 64], P(('batch', 'tm')), parts along dimension 0, may hold values 0 or 1
Outputs:
- state_step: float32 [512, 256], P(('batch', 'tm')), parts along dimension 0
- input_step: float32 [512, 64], P(('batch', 'tm')), parts along dimension 0
- multiplier_step: float32 [512, 256], P(('batch', 'tm')), parts along dimension 0
- bound_step: float32 [512, 64], P(('batch', 'tm')), parts along dimension 0
- kkt_norms: float32 [6], P('batch'), parts along dimension 0
There are 2 independent parts, one for each index of `batch`. A program takes and returns all parts, laid end to end along the dimension named above; each array names one. Nothing has to cross between parts.
Inputs may be any that keep to these rules, and one draw needn't show every extreme that they name: `value_matrix`: each section's matrix is symmetric. `gain_inverse`: each section's matrix is symmetric. `input_weight`: symmetric.
All inputs are finite; a program needn't handle non-finite values. No bound on the sum of `active` on one device may be relied on, other than what follows from the above.
Results may differ from a plain program's by a relative error of at most 0.0003.
Values sent between devices are 32-bit elements; how exact they have to be, the bound alone decides.
A program may use at most 128 MiB of HBM per device.

v0:
```python
import jax
import jax.numpy as jnp
from jax import lax
from jax.sharding import PartitionSpec as P

PRECISE = lax.Precision.HIGHEST
floor_share = 0.001


def shifted(x, axis, by):
    peers = lax.axis_size(axis)
    pairs = [(i, i + by) for i in range(peers) if 0 <= i + by < peers]
    return lax.ppermute(x, axis, pairs)


def carried_in(x, axis, combine, identity, reverse):
    peers, place = (lax.axis_size(axis), lax.axis_index(axis))
    everything = jax.tree.map(lambda part: lax.all_gather(part, axis), x)
    start = jax.tree.map(
        lambda part, zero: jnp.broadcast_to(jnp.asarray(zero, part.dtype), part.shape), x, identity
    )

    def turn(k, before):
        at = peers - 1 - k if reverse else k
        reached = at > place if reverse else at < place
        new = combine(before, jax.tree.map(lambda part: part[at], everything))
        return jax.tree.map(lambda a, b: jnp.where(reached, a, b), new, before)

    return lax.fori_loop(0, peers, turn, start)


def apply_each(matrices, vectors):
    return jnp.einsum("kij,kj->ki", matrices, vectors, precision=PRECISE)


def apply_transposed(matrices, vectors):
    return jnp.einsum("kji,kj->ki", matrices, vectors, precision=PRECISE)


def compose_block(loop_mats, sources):
    dimension = loop_mats.shape[-1]

    def compose_section(carried, section_item):
        product, costate = carried
        matrix, source = section_item
        return (
            (
                jnp.dot(product, matrix, precision=PRECISE),
                jnp.dot(costate, matrix, precision=PRECISE) + source,
            ),
            None,
        )

    start = (jnp.eye(dimension, dtype=jnp.float32), jnp.zeros((dimension,), jnp.float32))
    (product, costate), unused = lax.scan(
        compose_section, start, (loop_mats, sources), reverse=True
    )
    return (product, costate)


def backward_sweep(loop_mats, sources, incoming):

    def backward_section(costate, section_item):
        matrix, source = section_item
        earlier = jnp.dot(costate, matrix, precision=PRECISE) + source
        return (earlier, (costate, earlier))

    final_state, (after, before) = lax.scan(
        backward_section, incoming, (loop_mats, sources), reverse=True
    )
    return (after, before, final_state)


def forward_sweep(loop_mats, defects, pushes, entering):

    def forward_section(carried, section_item):
        matrix, defect, pushed = section_item
        correction = carried - defect
        return (jnp.dot(matrix, correction, precision=PRECISE) + pushed, correction)

    final_state, steps = lax.scan(forward_section, entering, (loop_mats, defects, pushes))
    return (steps, final_state)


def backward_join(earlier, latter):
    return (
        jnp.dot(earlier[0], latter[0], precision=PRECISE),
        jnp.dot(earlier[1], latter[0], precision=PRECISE) + latter[1],
    )


def forward_join(earlier, latter):
    return (
        jnp.dot(latter[0], earlier[0], precision=PRECISE),
        jnp.dot(latter[0], earlier[1], precision=PRECISE) + latter[1],
    )


def backward_join_sums(earlier, latter):
    joined = backward_join(earlier, latter)
    return (joined[0], joined[1], earlier[2] + latter[2])


def forward_join_sums(earlier, latter):
    joined = forward_join(earlier, latter)
    return (joined[0], joined[1], earlier[2] + latter[2])


def make_statistics(
    defect, grad_state, grad_input, slack_gap, offset, state_linear, input_linear, bound_mult
):
    return jnp.stack(
        [
            jnp.sum(defect * defect),
            jnp.sum(grad_state * grad_state) + jnp.sum(grad_input * grad_input),
            jnp.sum(slack_gap * slack_gap),
            jnp.sum(offset * offset),
            jnp.sum(state_linear * state_linear) + jnp.sum(input_linear * input_linear),
            jnp.sum(bound_mult * bound_mult),
        ]
    )


def make_norms(totals, horizon, state_count, input_count):
    primal = totals[0] / (totals[3] + floor_share * horizon * state_count)
    dual = totals[1] / (totals[4] + floor_share * horizon * (state_count + input_count))
    complement = totals[2] / (totals[5] + floor_share * horizon * input_count)
    return jnp.sqrt(jnp.stack([primal, dual, complement]))


def local(
    state_map,
    input_map,
    closed_loop,
    feedback,
    value_matrix,
    gain_inverse,
    input_weight,
    state_weight,
    state_linear,
    input_linear,
    offset,
    upper_bound,
    states,
    inputs,
    multipliers,
    bound_mult,
    active,
):
    state_count = states.shape[1]
    input_count = inputs.shape[1]
    devices = lax.axis_size("tm")
    horizon = states.shape[0] * devices
    predicted = apply_each(state_map, states) + apply_transposed(input_map, inputs)
    from_before = shifted(predicted[-1], "tm", 1)
    previous = jnp.concatenate([from_before[None], predicted[:-1]], axis=0)
    defect = states - previous - offset
    from_after = shifted(multipliers[0], "tm", -1)
    following = jnp.concatenate([multipliers[1:], from_after[None]], axis=0)
    grad_state = (
        state_weight * states + state_linear + multipliers - apply_transposed(state_map, following)
    )
    grad_input = (
        jnp.einsum("ij,kj->ki", input_weight, inputs, precision=PRECISE)
        + input_linear
        - apply_each(input_map, following)
        + bound_mult
    )
    slack_gap = bound_mult * (upper_bound - inputs)
    sources = apply_each(value_matrix, defect) + grad_state + apply_transposed(feedback, grad_input)
    statistics = make_statistics(
        defect, grad_state, grad_input, slack_gap, offset, state_linear, input_linear, bound_mult
    )
    product, local_costate = compose_block(closed_loop, sources)
    identity = jnp.eye(state_count, dtype=jnp.float32)
    empty_vector = jnp.zeros((state_count,), jnp.float32)
    empty_sums = jnp.zeros((6,), jnp.float32)
    incoming_map, incoming, above_sums = carried_in(
        (product, local_costate, statistics),
        "tm",
        backward_join_sums,
        (identity, empty_vector, empty_sums),
        True,
    )
    after, before, unused = backward_sweep(closed_loop, sources, incoming)
    pulled = apply_each(input_map, after)
    forward_gain = -apply_each(gain_inverse, grad_input + pulled)
    pushes = apply_transposed(input_map, forward_gain)
    unused_steps, local_state = forward_sweep(closed_loop, defect, pushes, empty_vector)
    entering_map, entering, below_sums = carried_in(
        (product, local_state, statistics),
        "tm",
        forward_join_sums,
        (identity, empty_vector, empty_sums),
        False,
    )
    totals = below_sums + statistics + above_sums
    state_step, final_state = forward_sweep(closed_loop, defect, pushes, entering)
    chosen = active.astype(jnp.float32)
    input_step = (1.0 - chosen) * (apply_each(feedback, state_step) + forward_gain) + chosen * (
        upper_bound - inputs
    )
    multiplier_step = apply_each(value_matrix, state_step - defect) + before
    bound_step = chosen * (
        grad_input + jnp.einsum("ij,kj->ki", input_weight, input_step, precision=PRECISE) + pulled
    )
    kkt_norms = make_norms(totals, horizon, state_count, input_count)
    return (state_step, input_step, multiplier_step, bound_step, kkt_norms)


def solution(mesh):
    in_specs = (
        P(("batch", "tm"), None, None),
        P(("batch", "tm"), None, None),
        P(("batch", "tm"), None, None),
        P(("batch", "tm"), None, None),
        P(("batch", "tm"), None, None),
        P(("batch", "tm"), None, None),
        P("batch", None),
        P(("batch", "tm"), None),
        P(("batch", "tm"), None),
        P(("batch", "tm"), None),
        P(("batch", "tm"), None),
        P(("batch", "tm"), None),
        P(("batch", "tm"), None),
        P(("batch", "tm"), None),
        P(("batch", "tm"), None),
        P(("batch", "tm"), None),
        P(("batch", "tm"), None),
    )
    out_specs = (
        P(("batch", "tm"), None),
        P(("batch", "tm"), None),
        P(("batch", "tm"), None),
        P(("batch", "tm"), None),
        P("batch"),
    )
    return jax.shard_map(local, mesh=mesh, in_specs=in_specs, out_specs=out_specs, check_vma=False)
```

profile of v0, /device:TPU:0, one launch (start us, length us, event | category | flops | bytes accessed | tf_op | source)
XLA Modules:
  0.0 338.4 jit_solution(11339350356689650067)
XLA Ops:
  8.0 1.3 collective-permute-start.1
  9.3 1.4 fusion.51
  10.7 5.9 %fusion.43 = f32[16,1,256]{2,1,0:T(1,128)S(1)} fusion(f32[16,256,256]{2,1,0:T(8,128)} %param.29, f32[16,256,1]{1,0,2:T(8,128)} %bitcast.259), kind=kOutput, calls=%fused_computation.77 | convolution fusion | flops 12582912 | bytes 4227072 | tf_op jit(solution)/shard_map/kij,kj->ki/dot_general | solution.py:33
  16.7 5.6 %collective-permute-start = (f32[256]{0:T(256)S(1)}, f32[256]{0:T(256)S(1)}, u32[]{:S(2)}, u32[]{:S(2)}) collective-permute-start(f32[256]{0:T(256)S(1)} %bitcast.272), channel_id=1, source_target_pairs={{0,2},{2,4},{4,6},{6,8},{8,10},{10,12},{12,14},{14,16},{16,18},{18... | collective-permute-start | bytes 3080 | tf_op jit(solution)/shard_map/ppermute | solution.py:13
  22.4 4.4 %fusion.47 = f32[16,1,256]{2,1,0:T(1,128)S(1)} fusion(f32[16,256,256]{2,1,0:T(8,128)} %param.29, f32[16,256,1]{1,0,2:T(8,128)S(1)} %maximum_bitcast_fusion), kind=kOutput, calls=%fused_computation.86 | convolution fusion | flops 12582912 | bytes 4227072 | tf_op jit(solution)/shard_map/kji,kj->ki/dot_general | solution.py:37
  30.0 3.5 %fusion.41 = f32[16,1,256]{2,1,0:T(1,128)S(1)} fusion(f32[16,256,256]{2,1,0:T(8,128)S(1)} %copy-done.1, f32[16,256,1]{1,0,2:T(8,128)S(1)} %bitcast.232), kind=kOutput, calls=%fused_computation.75 | convolution fusion | flops 12582912 | bytes 4227072 | tf_op jit(solution)/shard_map/kij,kj->ki/dot_general | solution.py:33
  33.6 45.5 %while.94 = (s32[]{:T(128)}, f32[256,256]{0,1:T(8,128)S(1)}, f32[256]{0:T(256)S(1)}, f32[16,256,256]{2,1,0:T(8,128)}, f32[16,256]{1,0:T(8,128)S(1)}, /*index=5*/s32[]{:T(128)}, s32[]{:T(128)}, s32[]{:T(128)}) while((s32[]{:T(128)}, f32[256,256]{0,1:T(8,128)S(1)}, f32[256]{0:T(256)S(1)}, f32[16,256,256]{2,1,0:T(8,128)}, ...), condition=%wide.region_1.0_spmd.clone, body=%wide.region_0.0_spmd.clone.sunk | while | flops 202113536 | bytes 1582207 | solution.py:55
  33.6 1.5 convolution_bitcast_fusion.2
  36.4 1.5 convolution_bitcast_fusion.2
  39.3 1.5 convolution_bitcast_fusion.2
  42.1 1.5 convolution_bitcast_fusion.2
  45.0 1.5 convolution_bitcast_fusion.2
  47.8 1.5 convolution_bitcast_fusion.2
  50.7 1.5 convolution_bitcast_fusion.2
  53.5 1.5 convolution_bitcast_fusion.2
  56.3 1.5 convolution_bitcast_fusion.2
  59.2 1.5 convolution_bitcast_fusion.2
  62.0 1.5 convolution_bitcast_fusion.2
  64.9 1.5 convolution_bitcast_fusion.2
  67.7 1.5 convolution_bitcast_fusion.2
  70.6 1.5 convolution_bitcast_fusion.2
  73.4 1.5 convolution_bitcast_fusion.2
  76.2 1.5 convolution_bitcast_fusion.2
  82.4 39.5 %all-gather.4 = f32[16,1,256]{2,1,0:T(1,128)S(1)} all-gather(f32[1,1,256]{2,1,0:T(1,128)S(1)} %bitcast.263), channel_id=3, replica_groups=mesh['tm'=16,'batch'=2] {'tm'}, dimensions={0}, use_global_device_ids=true | all-gather | bytes 17408 | tf_op jit(solution)/shard_map/all_gather | solution.py:18
  124.3 2.6 stack.33
  127.1 38.2 %all-reduce = f32[96]{0:T(128)S(1)} all-reduce(f32[96]{0:T(128)S(1)} %dynamic-update-slice), channel_id=4, replica_groups=mesh['tm'=16,'batch'=2] {'tm'}, use_global_device_ids=true, to_apply=%add | all-reduce | flops 96 | bytes 768
  165.4 5.6 %copy.24 = f32[4096,256]{1,0:T(8,128)} copy(f32[4096,256]{0,1:T(8,128)} %all-gather.8.cloned.1.call-done) | data formatting | bytes 8388608 | tf_op jit(solution)/shard_map/all_gather | solution.py:18
  171.0 20.7 %while.95 = (s32[]{:T(128)}, f32[256]{0:T(256)S(1)}, f32[6]{0:T(128)S(1)}, s32[]{:T(128)}, f32[16,256,256]{2,1,0:T(8,128)}, /*index=5*/f32[16,256]{1,0:T(8,128)S...) while((s32[]{:T(128)}, f32[256]{0:T(256)S(1)}, ...), condition=%wide.region_11.12_spmd.clone, body=%wide.region_10.11_spmd.clone.sunk | while | flops 787482 | bytes 272654 | solution.py:29
  191.7 21.3 %while.92 = (s32[]{:T(128)}, f32[256]{0:T(256)S(1)}, f32[16,256]{1,0:T(8,128)S(1)}, f32[16,256]{1,0:T(8,128)S(1)}, f32[16,256,256]{2,1,0:T(8,128)}, /*index=5*/f...) while((s32[]{:T(128)}, f32[256]{0:T(256)S(1)}, f32[16,256]{1,0:T(8,128)S(1)}, ...), condition=%wide.region_13.14_spmd, body=%wide.region_12.13_spmd.sunk | while | flops 786691 | bytes 273537 | solution.py:68
  215.6 21.1 %while.96 = (s32[]{:T(128)}, f32[256]{0:T(256)S(1)}, f32[16,256,256]{2,1,0:T(8,128)}, f32[16,256]{1,0:T(8,128)S(1)}, f32[16,256]{1,0:T(8,128)S(1)}, /*index=5*/s32[]{:T(128)}, s32[]{:T(128)}) while((s32[]{:T(128)}, f32[256]{0:T(256)S(1)}, f32[16,256,256]{2,1,0:T(8,128)}, f32[16,256]{1,0:T(8,128)S(1)}, f32[16,256]{1,0:T(8,128)S(1)}, ...), condition=%wide.region_15.16_spmd.clone, body=%wide.region_14.15_spmd.clone.sunk | while | flops 787203 | bytes 274535 | solution.py:81
  218.3 1.2 fusion.117
  219.6 1.2 fusion.117
  222.3 1.2 fusion.117
  223.6 1.2 fusion.117
  226.2 1.2 fusion.117
  227.6 1.2 fusion.117
  230.2 1.2 fusion.117
  231.5 1.2 fusion.117
  235.5 1.2 fusion.117
  236.8 37.8 %all-gather.5 = f32[16,1,256]{2,1,0:T(1,128)S(1)} all-gather(f32[1,1,256]{2,1,0:T(1,128)S(1)} %bitcast.262), channel_id=5, replica_groups=mesh['tm'=16,'batch'=2] {'tm'}, dimensions={0}, use_global_device_ids=true | all-gather | bytes 17408 | tf_op jit(solution)/shard_map/all_gather | solution.py:18
  274.6 21.8 %while.97 = (s32[]{:T(128)}, f32[256]{0:T(256)S(1)}, f32[6]{0:T(128)S(1)}, s32[]{:T(128)}, f32[16,256,256]{2,1,0:T(8,128)}, /*index=5*/f32[16,256]{1,0:T(8,128)S(1)}, f32[16,6]{1,0:T(8,128)S(1)}, s32[]{:T(128)}, s32[]{:T(128)}) while((s32[]{:T(128)}, f32[256]{0:T(256)S(1)}, f32[6]{0:T(128)S(1)}, s32[]{:T(128)}, ...), condition=%wide.region_17.18_spmd.clone, body=%wide.region_16.17_spmd.clone.sunk | while | flops 787478 | bytes 272592 | solution.py:29
  274.6 1.2 fusion.120
  280.0 1.2 fusion.120
  281.4 1.2 fusion.120
  282.8 1.2 fusion.120
  284.1 1.2 fusion.120
  296.4 22.0 %while.93 = (s32[]{:T(128)}, f32[256]{0:T(256)S(1)}, f32[16,256]{1,0:T(8,128)S(1)}, f32[16,256,256]{2,1,0:T(8,128)}, f32[16,256]{1,0:T(8,128)S(1)}, /*index=5*/f32[16,256]{1,0:T(8,128)S(1)}, s32[]{:T(128)}, s32[]{:T(128)}) while((s32[]{:T(128)}, f32[256]{0:T(256)S(1)}, f32[16,256]{1,0:T(8,128)S(1)}, f32[16,256,256]{2,1,0:T(8,128)}, ...), condition=%wide.region_19.20_spmd, body=%wide.region_18.19_spmd.sunk | while | flops 786946 | bytes 276585 | solution.py:81
  319.4 5.7 %fusion.35 = f32[16,1,256]{2,1,0:T(1,128)S(1)} fusion(f32[16,256,256]{2,1,0:T(8,128)} %param.33, f32[16,256,1]{1,0,2:T(8,128)S(1)} %subtract_bitcast_fusion), kind=kOutput, calls=%fused_computation.68 | convolution fusion | flops 12582912 | bytes 4227072 | tf_op jit(solution)/shard_map/kij,kj->ki/dot_general | solution.py:33
  (535 shorter events, 118.0 us)
Async XLA Ops:
  7.2 2.1 copy-start
  7.2 15.2 %copy-start.8 = (f32[16,256]{1,0:T(8,128)S(1)}, f32[16,256]{1,0:T(8,128)}, u32[]{:S(2)}) copy-start(f32[16,256]{1,0:T(8,128)} %param.43) | copy-start | bytes 49156
  7.2 158.2 %all-gather.8.cloned.1.call-start = ((), (), s32[]{:S(2)}) async-start(), calls=%async_computation | async-start | bytes 4456448 | tf_op jit(solution)/shard_map/all_gather | solution.py:18
  8.0 14.4 %collective-permute-start.1 = (f32[256]{0:T(256)S(1)}, f32[256]{0:T(256)S(1)}, u32[]{:S(2)}, u32[]{:S(2)}) collective-permute-start(f32[256]{0:T(256)S(1)} %bitcast.273), channel_id=1, source_target_pairs={{2,0},{4,2},{6,4},{8,6},{10,8},{12,10},{14,12},{16,14},{18,16},{20... | collective-permute-start | bytes 3080 | tf_op jit(solution)/shard_map/ppermute | solution.py:13
  10.7 17.1 %copy-start.6 = (f32[16,64]{1,0:T(8,128)S(1)}, f32[16,64]{1,0:T(8,128)}, u32[]{:S(2)}) copy-start(f32[16,64]{1,0:T(8,128)} %param.42) | copy-start | bytes 12292
  10.7 17.1 %copy-start.7 = (f32[64,64]{1,0:T(8,128)S(1)}, f32[64,64]{1,0:T(8,128)}, u32[]{:S(2)}) copy-start(f32[64,64]{1,0:T(8,128)} %param.35) | copy-start | bytes 49156
  10.7 17.1 %copy-start.10 = (f32[16,64]{1,0:T(8,128)S(1)}, f32[16,64]{1,0:T(8,128)}, u32[]{:S(2)}) copy-start(f32[16,64]{1,0:T(8,128)} %param.44) | copy-start | bytes 12292
  10.7 17.1 %copy-start.11 = (f32[16,64]{1,0:T(8,128)S(1)}, f32[16,64]{1,0:T(8,128)}, u32[]{:S(2)}) copy-start(f32[16,64]{1,0:T(8,128)} %param.38) | copy-start | bytes 12292
  10.7 17.9 %copy-start.3 = (f32[16,64,256]{2,1,0:T(8,128)S(1)}, f32[16,64,256]{2,1,0:T(8,128)}, u32[]{:S(2)}) copy-start(f32[16,64,256]{2,1,0:T(8,128)} %param.32) | copy-start | bytes 3145732
  16.6 12.6 %copy-start.9 = (f32[16,256]{1,0:T(8,128)S(1)}, f32[16,256]{1,0:T(8,128)}, u32[]{:S(2)}) copy-start(f32[16,256]{1,0:T(8,128)} %param.41) | copy-start | bytes 49156
  16.6 12.6 %copy-start.15 = (f32[16,256]{1,0:T(8,128)S(1)}, f32[16,256]{1,0:T(8,128)}, u32[]{:S(2)}) copy-start(f32[16,256]{1,0:T(8,128)} %param.37) | copy-start | bytes 49156
  16.6 12.7 %copy-start.16 = (f32[16,256]{1,0:T(8,128)S(1)}, f32[16,256]{1,0:T(8,128)}, u32[]{:S(2)}) copy-start(f32[16,256]{1,0:T(8,128)} %param.36) | copy-start | bytes 49156
  16.6 12.6 %copy-start.17 = (f32[16,256]{1,0:T(8,128)S(1)}, f32[16,256]{1,0:T(8,128)}, u32[]{:S(2)}) copy-start(f32[16,256]{1,0:T(8,128)} %param.39) | copy-start | bytes 49156
  16.7 12.6 %collective-permute-start = (f32[256]{0:T(256)S(1)}, f32[256]{0:T(256)S(1)}, u32[]{:S(2)}, u32[]{:S(2)}) collective-permute-start(f32[256]{0:T(256)S(1)} %bitcast.272), channel_id=1, source_target_pairs={{0,2},{2,4},{4,6},{6,8},{8,10},{10,12},{12,14},{14,16},{16,18},{18... | collective-permute-start | bytes 3080 | tf_op jit(solution)/shard_map/ppermute | solution.py:13
  22.4 7.6 %copy-start.1 = (f32[16,256,256]{2,1,0:T(8,128)S(1)}, f32[16,256,256]{2,1,0:T(8,128)}, u32[]{:S(2)}) copy-start(f32[16,256,256]{2,1,0:T(8,128)} %param.33) | copy-start | bytes 12582916
  33.5 46.3 %copy-start.18 = (u32[32]{0:T(128)S(1)}, u32[32]{0:T(128)}, u32[]{:S(2)}) copy-start(u32[32]{0:T(128)} %constant.198) | copy-start | bytes 388
  33.5 48.1 %copy-start.12 = (f32[16,64]{1,0:T(8,128)S(1)}, f32[16,64]{1,0:T(8,128)}, u32[]{:S(2)}) copy-start(f32[16,64]{1,0:T(8,128)} %param.40) | copy-start | bytes 12292
  79.0 0.7 copy-start.2
  171.0 43.0 %copy-start.4 = (f32[16,64,64]{2,1,0:T(8,128)S(1)}, f32[16,64,64]{2,1,0:T(8,128)}, u32[]{:S(2)}) copy-start(f32[16,64,64]{2,1,0:T(8,128)} %param.34) | copy-start | bytes 786436
  274.6 50.5 %copy-start.13 = (s32[16,64]{1,0:T(8,128)S(1)}, s32[16,64]{1,0:T(8,128)}, u32[]{:S(2)}) copy-start(s32[16,64]{1,0:T(8,128)} %param.45) | copy-start | bytes 12292
  318.4 13.1 %copy-start.5 = (f32[16,256]{1,0:T(8,128)}, f32[16,256]{1,0:T(8,128)S(1)}, u32[]{:S(2)}) copy-start(f32[16,256]{1,0:T(8,128)S(1)} %get-tuple-element.588) | copy-start | bytes 49156
  325.1 6.4 %copy-start.14 = (f32[16,64]{1,0:T(8,128)}, f32[16,64]{1,0:T(8,128)S(1)}, u32[]{:S(2)}) copy-start(f32[16,64]{1,0:T(8,128)S(1)} %multiply_add_fusion) | copy-start | bytes 12292
Sparse Core Ops, SparseCore 0:
  79.9 83.6 all-gather.7
where the time goes:
time: 342 us; the launch traced here: 338 us
  matrix products  167 us (49%)
  blocking collectives  115 us (34%)
  between operations  21.3 us (6%)
  local copies, waits for them, and re-layouts  16.8 us (5%)
  starting transfers between devices  6.95 us (2%)
  loops' own time  5.7 us (2%)
  other arithmetic  5.03 us (1%)
    all_gather x2, blocking collectives, carried_in(): everything = jax.tree.map(lambda part: lax.all_gather(part, axis), x)  77.3 us
    dot_general x32, matrix products, forward_section(): return (jnp.dot(matrix, correction, precision=PRECISE) + pushed, correction)  39.2 us
    unnamed x1, blocking collectives  38.2 us
    dot_general x16, matrix products, compose_section(): jnp.dot(product, matrix, precision=PRECISE)  24.8 us
    dot_general x16, matrix products, forward_join(): jnp.dot(latter[0], earlier[1], precision=PRECISE) + latter[1]  19.6 us
    dot_general x7, matrix products, apply_each(): return jnp.einsum('kij,kj->ki', matrices, vectors, precision=PRECISE)  18.9 us
    dot_general x16, matrix products, backward_join(): jnp.dot(earlier[1], latter[0], precision=PRECISE) + latter[1]  18.7 us
    dot_general x16, matrix products, compose_section(): jnp.dot(costate, matrix, precision=PRECISE) + source  18.7 us
  transfers between devices with their start and end apart: 3, of which 0 were waited for; matrix products, arithmetic and copies ran while one was open for 6% of the time, Pallas kernels for 0%

commit v1 on v0

v1 whole, which is shorter than its diff:
```python
import functools
import jax
import jax.numpy as jnp
from jax import lax
from jax.experimental import pallas as pl
from jax.experimental.pallas import tpu as pltpu
from jax.sharding import PartitionSpec as P

F32 = jnp.float32
BF16 = jnp.bfloat16
PRECISE = lax.Precision.HIGHEST
MESH = pl.DeviceIdType.MESH
floor_share = 0.001
LANES = 128


def parts_of(x):
    high = x.astype(BF16)
    return high, (x - high.astype(F32)).astype(BF16)


def matmul(a, b):
    ah, al = parts_of(a)
    bh, bl = parts_of(b)
    dot = functools.partial(jnp.dot, preferred_element_type=F32)
    return dot(ah, bh) + (dot(ah, bl) + dot(al, bh))


def turned(x):
    rows, cols = x.shape
    up = -rows % LANES
    side = -cols % LANES
    if up:
        x = jnp.concatenate([x, jnp.zeros((up, cols), F32)], axis=0)
    if side:
        x = jnp.concatenate([x, jnp.zeros((rows + up, side), F32)], axis=1)
    return x.T[:cols, :rows]


def column(row):
    return jnp.broadcast_to(row, (LANES, row.shape[1])).T[:, :1]


def row_of(col):
    return jnp.broadcast_to(col, (col.shape[0], LANES)).T[:1]


def times(matrix, row):
    return jnp.sum(matrix * row, axis=1, keepdims=True)


def times_t(matrix, col):
    return jnp.sum(matrix * col, axis=0, keepdims=True)


def kernel(n, size, *refs):
    (a_hbm, b_hbm, m_hbm, k_hbm, v_hbm, gi_hbm, w_hbm, sw_hbm, sl_hbm, il_hbm, of_hbm, ub_hbm,
     st_hbm, in_hbm, mu_hbm, bm_hbm, ac_hbm,
     o_state, o_input, o_mult, o_bound, o_norm,
     a, b, m, fb, v, gi, w, sw, sl, il, of, ub, st, inp, mu, bm, ac,
     pre, suf, group, whole, sources, pushes, back_local, fwd_local, back,
     cols, fol_in, prd_in, prd_out, fol_out, vec_b, vec_f, ch_b_in, ch_f_in, ch_b_out, ch_f_out,
     load_sem, m_sem, nb_send, nb_recv, p_send, p_recv, b_send, b_recv, f_send, f_recv,
     ch_send, ch_recv) = refs
    me = lax.axis_index("tm")
    place = lax.rem(me, size)
    base = me - place
    at_group = lax.div(me, size)
    groups = n // size
    sections, ns = st.shape
    nu = inp.shape[1]
    half = sections // 2

    order = []
    for i in range(half):
        order += [i, sections - 1 - i]
    for k in order:
        pltpu.make_async_copy(m_hbm.at[k], m.at[k], m_sem.at[k]).start()
    small = [(w_hbm, w), (sw_hbm, sw), (sl_hbm, sl), (il_hbm, il), (of_hbm, of), (ub_hbm, ub),
             (st_hbm, st), (in_hbm, inp), (mu_hbm, mu), (bm_hbm, bm), (ac_hbm, ac)]
    large = [(a_hbm, a), (b_hbm, b), (v_hbm, v), (k_hbm, fb), (gi_hbm, gi)]
    loads = [
        pltpu.make_async_copy(src, dst, load_sem.at[i]) for i, (src, dst) in enumerate(small + large)
    ]
    for load in loads:
        load.start()

    barrier = pltpu.get_barrier_semaphore()
    first_of, last_of = place == 0, place == size - 1
    relations = [
        (jnp.logical_and(first_of, me > 0), me - 1),
        (jnp.logical_and(last_of, me < n - 1), me + 1),
        (at_group > 0, me - size),
        (at_group < groups - 1, me + size),
    ]
    mates = [base + lax.rem(place + j, size) for j in range(1, size)]
    for mate in mates:
        pl.semaphore_signal(barrier, inc=1, device_id={"tm": mate}, device_id_type=MESH)
    for holds, peer in relations:
        @pl.when(holds)
        def _():
            pl.semaphore_signal(barrier, inc=1, device_id={"tm": peer}, device_id_type=MESH)
    peers = size - 1
    for holds, peer in relations:
        peers = peers + jnp.where(holds, 1, 0)
    pl.semaphore_wait(barrier, peers)

    def remote(src, dst, send, recv, peer):
        return pltpu.make_async_remote_copy(
            src_ref=src, dst_ref=dst, send_sem=send, recv_sem=recv,
            device_id={"tm": peer}, device_id_type=MESH,
        )

    for load in loads[: len(small)]:
        load.wait()
    to_earlier = remote(fol_out, fol_in, nb_send.at[0], nb_recv.at[0], me - 1)
    to_later = remote(prd_out, prd_in, nb_send.at[1], nb_recv.at[1], me + 1)
    fol_out[...] = jnp.broadcast_to(mu[0:1], fol_out.shape)

    @pl.when(me > 0)
    def _():
        to_earlier.start()

    def wait_loop(k):
        pltpu.make_async_copy(m_hbm.at[k], m.at[k], m_sem.at[k]).wait()

    wait_loop(0)
    wait_loop(sections - 1)
    pre[0] = m[0]
    suf[sections - 1] = m[sections - 1]

    def grow(i, waits):
        j = sections - 1 - i
        if waits:
            wait_loop(i)
            wait_loop(j)
        pre[i] = matmul(m[i], pre[i - 1])
        suf[j] = matmul(suf[j + 1], m[j])

    @pl.loop(1, half)
    def _(i):
        grow(i, True)

    product = matmul(suf[half], pre[half - 1])
    suf[0] = product
    group[pl.ds(place, 1)] = product[None]
    p_copies = [
        remote(group.at[place], group.at[place], p_send.at[j], p_recv.at[j], mate)
        for j, mate in enumerate(mates)
    ]
    for copy in p_copies:
        copy.start()

    for load in loads[len(small):]:
        load.wait()
    lane = lax.broadcasted_iota(jnp.int32, (ns, LANES), 1)
    lane_u = lax.broadcasted_iota(jnp.int32, (nu, LANES), 1)

    inputs_t = turned(inp[...])
    acc = jnp.zeros((ns, LANES), F32)
    for k in range(sections):
        acc = jnp.where(lane == k, times(a[k], st[k:k + 1]), acc)
    predicted = acc.T[:sections]
    rows = [times_t(b[k], inputs_t[:, k:k + 1]) for k in range(sections)]
    predicted = predicted + jnp.concatenate(rows, axis=0)
    prd_out[...] = jnp.broadcast_to(predicted[sections - 1:], prd_out.shape)

    @pl.when(me < n - 1)
    def _():
        to_later.start()

    @pl.loop(half, sections - 1)
    def _(i):
        grow(i, False)

    @pl.when(me < n - 1)
    def _():
        to_earlier.wait_recv()

    @pl.when(me == n - 1)
    def _():
        fol_in[...] = jnp.zeros_like(fol_in)

    following = jnp.concatenate([mu[1:], fol_in[0:1]], axis=0)
    following_t = turned(following)
    grad_input = (
        jnp.dot(inp[...], w[...], precision=PRECISE, preferred_element_type=F32) + il[...] + bm[...]
    )
    acc = jnp.zeros((nu, LANES), F32)
    for k in range(sections):
        acc = jnp.where(lane_u == k, times(b[k], following[k:k + 1]), acc)
    grad_input = grad_input - turned(acc)[:sections]
    grad_input_t = turned(grad_input)
    rows = [times_t(a[k], following_t[:, k:k + 1]) for k in range(sections)]
    grad_state = sw[...] * st[...] + sl[...] + mu[...] - jnp.concatenate(rows, axis=0)

    @pl.when(me > 0)
    def _():
        to_later.wait_recv()

    @pl.when(me == 0)
    def _():
        prd_in[...] = jnp.zeros_like(prd_in)

    previous = jnp.concatenate([prd_in[0:1], predicted[:sections - 1]], axis=0)
    defect = st[...] - previous - of[...]
    defect_t = turned(defect)
    rows = [
        times_t(v[k], defect_t[:, k:k + 1]) + times_t(fb[k], grad_input_t[:, k:k + 1])
        for k in range(sections)
    ]
    sources[...] = jnp.concatenate(rows, axis=0) + grad_state
    slack = bm[...] * (ub[...] - inp[...])

    def total(*xs):
        return sum(
            jnp.sum(jnp.sum(x * x, axis=1, keepdims=True), axis=0, keepdims=True) for x in xs
        )

    sums = [total(defect), total(grad_state, grad_input), total(slack), total(of[...]),
            total(sl[...], il[...]), total(bm[...])]
    line = lax.broadcasted_iota(jnp.int32, (1, ns), 1)
    stats = jnp.zeros((1, ns), F32)
    for i, value in enumerate(sums):
        stats = jnp.where(line == i, value, stats)

    def packed(vector, extra):
        return jnp.concatenate([vector, extra, jnp.zeros((6, ns), F32)], axis=0)

    costate = sources[sections - 1:]
    back_local[sections - 1:] = costate
    for k in range(sections - 2, -1, -1):
        costate = times_t(m[k], column(costate)) + sources[k:k + 1]
        back_local[k:k + 1] = costate
    vec_b[pl.ds(place, 1)] = packed(costate, stats)[None]
    b_copies = [
        remote(vec_b.at[place], vec_b.at[place], b_send.at[j], b_recv.at[j], mate)
        for j, mate in enumerate(mates)
    ]
    for copy in b_copies:
        copy.start()

    def arrive(buffer, send, recv):
        for j in range(size - 1):
            source = base + lax.rem(place + size - 1 - j, size)
            slot = source - base
            remote(buffer.at[slot], buffer.at[slot], send.at[j], recv.at[j], source).wait_recv()

    arrive(vec_b, b_send, b_recv)
    arrive(group, p_send, p_recv)
    joined = group[0]
    for e in range(1, size):
        joined = matmul(group[e], joined)
    whole[...] = joined
    group_stats = jnp.sum(vec_b[:, 1, :], axis=0, keepdims=True)

    y = vec_b[size - 1, 0:1]
    for e in range(size - 2, -1, -1):
        y = vec_b[e, 0:1] + times_t(group[e], column(y))
    to_before = remote(ch_b_out, ch_b_in, ch_send.at[0], ch_recv.at[0], me - size)
    to_after = remote(ch_f_out, ch_f_in, ch_send.at[1], ch_recv.at[1], me + size)

    @pl.when(at_group < groups - 1)
    def _():
        to_before.wait_recv()

    @pl.when(at_group == groups - 1)
    def _():
        ch_b_in[...] = jnp.zeros_like(ch_b_in)

    incoming = ch_b_in[0:1]
    above = ch_b_in[1:2]
    ch_b_out[...] = packed(times_t(whole[...], column(incoming)) + y, above + group_stats)

    @pl.when(at_group > 0)
    def _():
        to_before.start()

    for e in range(size - 1, 0, -1):
        new = vec_b[e, 0:1] + times_t(group[e], column(incoming))
        incoming = jnp.where(place < e, new, incoming)

    incoming_c = column(incoming)
    for k in range(sections):
        back[k:k + 1] = times_t(suf[k], incoming_c) + back_local[k:k + 1]
    before = back[...]
    after = jnp.concatenate([before[1:], incoming], axis=0)
    acc = jnp.zeros((nu, LANES), F32)
    for k in range(sections):
        acc = jnp.where(lane_u == k, times(b[k], after[k:k + 1]), acc)
    pulled = turned(acc)[:sections]
    held = grad_input + pulled
    acc = jnp.zeros((nu, LANES), F32)
    for k in range(sections):
        gain = -times(gi[k], held[k:k + 1])
        acc = jnp.where(lane_u == k, gain, acc)
        pushes[k:k + 1] = times_t(b[k], gain)
    forward_gain = turned(acc)[:sections]

    acc = jnp.zeros((ns, ns), F32)
    for k in range(sections):
        drive = -defect[k:k + 1]
        if k:
            drive = drive + pushes[k - 1:k]
        acc = acc + suf[k] * drive
    ended = row_of(jnp.sum(acc, axis=1, keepdims=True)) + pushes[sections - 1:]
    vec_f[pl.ds(place, 1)] = packed(ended, stats)[None]
    f_copies = [
        remote(vec_f.at[place], vec_f.at[place], f_send.at[j], f_recv.at[j], mate)
        for j, mate in enumerate(mates)
    ]
    for copy in f_copies:
        copy.start()

    step = -defect[0:1]
    acc = jnp.where(lane == 0, column(step), 0.0)
    for k in range(1, sections):
        moved = times(m[k - 1], step)
        step = row_of(moved) + pushes[k - 1:k] - defect[k:k + 1]
        acc = jnp.where(lane == k, column(step), acc)
    cols[...] = acc

    arrive(vec_f, f_send, f_recv)
    y = vec_f[0, 0:1]
    for e in range(1, size):
        y = vec_f[e, 0:1] + row_of(times(group[e], y))

    @pl.when(at_group > 0)
    def _():
        to_after.wait_recv()

    @pl.when(at_group == 0)
    def _():
        ch_f_in[...] = jnp.zeros_like(ch_f_in)

    entering = ch_f_in[0:1]
    below = ch_f_in[1:2]
    ch_f_out[...] = packed(row_of(times(whole[...], entering)) + y, below + group_stats)

    @pl.when(at_group < groups - 1)
    def _():
        to_after.start()

    for e in range(size - 1):
        new = vec_f[e, 0:1] + row_of(times(group[e], entering))
        entering = jnp.where(place > e, new, entering)

    acc = cols[...] + jnp.where(lane == 0, column(entering), 0.0)
    for k in range(1, sections):
        acc = acc + jnp.where(lane == k, times(pre[k - 1], entering), 0.0)
    state_step = acc.T[:sections]
    o_state[...] = state_step
    moved = acc[:, :sections] - defect_t
    for k in range(sections):
        o_mult[k:k + 1] = times_t(v[k], moved[:, k:k + 1]) + back[k:k + 1]
    acc = jnp.zeros((nu, LANES), F32)
    for k in range(sections):
        acc = jnp.where(lane_u == k, times(fb[k], state_step[k:k + 1]), acc)
    fed = turned(acc)[:sections]
    chosen = ac[...].astype(F32)
    input_step = (1.0 - chosen) * (fed + forward_gain) + chosen * (ub[...] - inp[...])
    o_input[...] = input_step
    o_bound[...] = chosen * (
        held + jnp.dot(input_step, w[...], precision=PRECISE, preferred_element_type=F32)
    )
    totals = above + group_stats + below
    tops = totals[:, 0:3]
    scale = totals[:, 3:6]
    spot = lax.broadcasted_iota(jnp.int32, (1, 3), 1)
    horizon = sections * n
    entries = jnp.where(spot == 0, ns, jnp.where(spot == 1, ns + nu, nu)).astype(F32)
    o_norm[...] = jnp.sqrt(tops / (scale + floor_share * horizon * entries))

    @pl.when(me > 0)
    def _():
        to_earlier.wait_send()

    @pl.when(me < n - 1)
    def _():
        to_later.wait_send()

    for copy in p_copies + b_copies + f_copies:
        copy.wait_send()

    @pl.when(at_group > 0)
    def _():
        to_before.wait_send()

    @pl.when(at_group < groups - 1)
    def _():
        to_after.wait_send()


def local(n, *args):
    size = 4 if n % 4 == 0 else (2 if n % 2 == 0 else 1)
    sections, ns = args[12].shape
    nu = args[13].shape[1]
    mates = size - 1
    copies = [pltpu.VMEM(x.shape, x.dtype) for x in args]
    message = (8, ns)
    dma = pltpu.SemaphoreType.DMA
    scratch = copies + [
        pltpu.VMEM((sections, ns, ns), F32),
        pltpu.VMEM((sections, ns, ns), F32),
        pltpu.VMEM((size, ns, ns), F32),
        pltpu.VMEM((ns, ns), F32),
        pltpu.VMEM((sections, ns), F32),
        pltpu.VMEM((sections, ns), F32),
        pltpu.VMEM((sections, ns), F32),
        pltpu.VMEM((sections, ns), F32),
        pltpu.VMEM((sections, ns), F32),
        pltpu.VMEM((ns, LANES), F32),
    ] + [pltpu.VMEM(message, F32)] * 4 + [
        pltpu.VMEM((size,) + message, F32),
        pltpu.VMEM((size,) + message, F32),
    ] + [pltpu.VMEM(message, F32)] * 4 + [
        dma((16,)), dma((sections,)), dma((2,)), dma((2,)),
        dma((mates,)), dma((mates,)), dma((mates,)), dma((mates,)), dma((mates,)), dma((mates,)),
        dma((2,)), dma((2,)),
    ]
    outs = [(sections, ns), (sections, nu), (sections, ns), (sections, nu), (1, 3)]
    results = pl.pallas_call(
        functools.partial(kernel, n, size),
        out_shape=[jax.ShapeDtypeStruct(shape, F32) for shape in outs],
        in_specs=[pl.BlockSpec(memory_space=pl.ANY)] * len(args),
        out_specs=[pl.BlockSpec(memory_space=pltpu.VMEM)] * len(outs),
        scratch_shapes=scratch,
        compiler_params=pltpu.CompilerParams(
            collective_id=0, has_side_effects=True, vmem_limit_bytes=60 * 1024 * 1024
        ),
    )(*args)
    return (*results[:4], results[4][0])


def solution(mesh):
    wide = P(("batch", "tm"), None, None)
    flat = P(("batch", "tm"), None)
    in_specs = (wide,) * 6 + (P("batch", None),) + (flat,) * 10
    out_specs = (flat,) * 4 + (P("batch"),)
    return jax.shard_map(
        functools.partial(local, mesh.shape["tm"]),
        mesh=mesh, in_specs=in_specs, out_specs=out_specs, check_vma=False,
    )
```

time: 342 us -> 62.1 us (0.18)
  the two profiles are of different devices: /device:TPU:0 before, /device:TPU:24 now
where the time goes in v1:
time: 62.1 us; the launch traced here: 61.6 us
  Pallas kernels  54.6 us (88%)
  local copies, waits for them, and re-layouts  6.35 us (10%)
  between operations  0.65 us (1%)
    pallas_call x1, Pallas kernels, local(): pl.pallas_call(functools.partial(kernel, n, size), out_shape=[jax.ShapeDt...  54.6 us
    unnamed x5, local copies, waits for them, and re-layouts  6.35 us

profile of v1, /device:TPU:24, one launch (start us, length us, event | category | flops | bytes accessed | tf_op | source)
XLA Modules:
  0.0 61.6 jit_solution(4406301282065268268)
XLA Ops:
  0.6 54.6 %shard_map.200 = (f32[16,256]{1,0:T(8,128)}, f32[16,64]{1,0:T(8,128)}, f32[16,256]{1,0:T(8,128)}, f32[16,64]{1,0:T(8,128)}, f32[1,3]{1,0:T(1,128)}) custom-call(f32[16,256,256]{2,1,0:T(8,128)} %refs_0_.1, f32[16,64,256]{2,1,0:T(8,128)} %refs_1_.1, f32[16,256,256]{2,1,0:T(8,128)} %refs_2_.1, f32[16,64,256]{2,1,0:T(8,128)} %refs_3_.1, ...), custom_call_target="tpu_custom_call" | custom-call | tf_op jit(solution)/shard_map/pallas_call | solution.py:422
  55.2 1.3 %copy.27 = f32[16,256]{1,0:T(8,128)} copy(f32[16,256]{1,0:T(8,128)} %get-tuple-element.20) | data formatting | bytes 32768
  56.6 1.3 %copy.28 = f32[16,64]{1,0:T(8,128)} copy(f32[16,64]{1,0:T(8,128)} %get-tuple-element.21) | data formatting | bytes 8192
  57.9 1.3 %copy.29 = f32[16,256]{1,0:T(8,128)} copy(f32[16,256]{1,0:T(8,128)} %get-tuple-element.22) | data formatting | bytes 32768
  59.2 1.3 %copy.30 = f32[16,64]{1,0:T(8,128)} copy(f32[16,64]{1,0:T(8,128)} %get-tuple-element.23) | data formatting | bytes 8192
  60.5 1.1 %copy.31 = f32[3]{0:T(128)} copy(f32[3]{0:T(128)} %bitcast.1) | data formatting | bytes 24

commit v2 on v1

--- a/solution.py
+++ b/solution.py
@@ -100,11 +100,6 @@
         @pl.when(holds)
         def _():
             pl.semaphore_signal(barrier, inc=1, device_id={"tm": peer}, device_id_type=MESH)
-    peers = size - 1
-    for holds, peer in relations:
-        peers = peers + jnp.where(holds, 1, 0)
-    pl.semaphore_wait(barrier, peers)
-
     def remote(src, dst, send, recv, peer):
         return pltpu.make_async_remote_copy(
             src_ref=src, dst_ref=dst, send_sem=send, recv_sem=recv,
@@ -116,10 +111,6 @@
     to_earlier = remote(fol_out, fol_in, nb_send.at[0], nb_recv.at[0], me - 1)
     to_later = remote(prd_out, prd_in, nb_send.at[1], nb_recv.at[1], me + 1)
     fol_out[...] = jnp.broadcast_to(mu[0:1], fol_out.shape)
-
-    @pl.when(me > 0)
-    def _():
-        to_earlier.start()
 
     def wait_loop(k):
         pltpu.make_async_copy(m_hbm.at[k], m.at[k], m_sem.at[k]).wait()
@@ -144,10 +135,33 @@
     product = matmul(suf[half], pre[half - 1])
     suf[0] = product
     group[pl.ds(place, 1)] = product[None]
-    p_copies = [
-        remote(group.at[place], group.at[place], p_send.at[j], p_recv.at[j], mate)
-        for j, mate in enumerate(mates)
-    ]
+    peers = size - 1
+    for holds, peer in relations:
+        peers = peers + jnp.where(holds, 1, 0)
+    pl.semaphore_wait(barrier, peers)
+
+    @pl.when(me > 0)
+    def _():
+        to_earlier.start()
+
+    along = place + 1 - 2 * lax.rem(place, 2)
+    across = place + 2 - 4 * lax.div(place, 2)
+    far = size - 1 - place
+    top, bottom = pl.ds(0, ns // 2), pl.ds(ns // 2, ns // 2)
+
+    def whole_block(slot, j, peer):
+        return remote(group.at[slot], group.at[slot], p_send.at[j], p_recv.at[j], base + peer)
+
+    def half_block(slot, rows, j, peer):
+        ref = group.at[slot, rows]
+        return remote(ref, ref, p_send.at[j], p_recv.at[j], base + peer)
+
+    if size == 4:
+        p_copies = [whole_block(place, 0, along), whole_block(place, 1, across)]
+    else:
+        p_copies = [
+            whole_block(place, j, lax.rem(place + j + 1, size)) for j in range(size - 1)
+        ]
     for copy in p_copies:
         copy.start()
 
@@ -227,27 +241,45 @@
     def packed(vector, extra):
         return jnp.concatenate([vector, extra, jnp.zeros((6, ns), F32)], axis=0)
 
+    sources_t = turned(sources[...])
+    costate = sources[0:1]
+    for k in range(1, sections):
+        costate = costate + times_t(pre[k - 1], sources_t[:, k:k + 1])
+    vec_b[pl.ds(place, 1)] = packed(costate, stats)[None]
+    b_copies = [
+        remote(vec_b.at[place], vec_b.at[place], b_send.at[j], b_recv.at[j], mate)
+        for j, mate in enumerate(mates)
+    ]
+    for copy in b_copies:
+        copy.start()
+
+    def arrive(buffer, send, recv):
+        for j in range(size - 1):
+            source = base + lax.rem(place + size - 1 - j, size)
+            slot = source - base
+            remote(buffer.at[slot], buffer.at[slot], send.at[j], recv.at[j], source).wait_recv()
+
+    if size == 4:
+        whole_block(along, 0, along).wait_recv()
+        second = half_block(along, top, 2, across)
+        second.start()
+        whole_block(across, 1, across).wait_recv()
+        third = half_block(across, bottom, 3, along)
+        third.start()
+        p_copies = p_copies + [second, third]
+
     costate = sources[sections - 1:]
     back_local[sections - 1:] = costate
     for k in range(sections - 2, -1, -1):
         costate = times_t(m[k], column(costate)) + sources[k:k + 1]
         back_local[k:k + 1] = costate
-    vec_b[pl.ds(place, 1)] = packed(costate, stats)[None]
-    b_copies = [
-        remote(vec_b.at[place], vec_b.at[place], b_send.at[j], b_recv.at[j], mate)
-        for j, mate in enumerate(mates)
-    ]
-    for copy in b_copies:
-        copy.start()
-
-    def arrive(buffer, send, recv):
-        for j in range(size - 1):
-            source = base + lax.rem(place + size - 1 - j, size)
-            slot = source - base
-            remote(buffer.at[slot], buffer.at[slot], send.at[j], recv.at[j], source).wait_recv()
 
     arrive(vec_b, b_send, b_recv)
-    arrive(group, p_send, p_recv)
+    if size == 4:
+        half_block(far, top, 2, across).wait_recv()
+        half_block(far, bottom, 3, along).wait_recv()
+    else:
+        arrive(group, p_send, p_recv)
     joined = group[0]
     for e in range(1, size):
         joined = matmul(group[e], joined)
@@ -312,13 +344,18 @@
     for copy in f_copies:
         copy.start()
 
-    step = -defect[0:1]
-    acc = jnp.where(lane == 0, column(step), 0.0)
-    for k in range(1, sections):
-        moved = times(m[k - 1], step)
-        step = row_of(moved) + pushes[k - 1:k] - defect[k:k + 1]
-        acc = jnp.where(lane == k, column(step), acc)
-    cols[...] = acc
+    def forward_alone():
+        step = -defect[0:1]
+        acc = jnp.where(lane == 0, column(step), 0.0)
+        for k in range(1, sections):
+            moved = times(m[k - 1], step)
+            step = row_of(moved) + pushes[k - 1:k] - defect[k:k + 1]
+            acc = jnp.where(lane == k, column(step), acc)
+        cols[...] = acc
+
+    @pl.when(at_group > 0)
+    def _():
+        forward_alone()
 
     arrive(vec_f, f_send, f_recv)
     y = vec_f[0, 0:1]
@@ -340,6 +377,10 @@
     @pl.when(at_group < groups - 1)
     def _():
         to_after.start()
+
+    @pl.when(at_group == 0)
+    def _():
+        forward_alone()
 
     for e in range(size - 1):
         new = vec_f[e, 0:1] + row_of(times(group[e], entering))
@@ -415,7 +456,7 @@
         pltpu.VMEM((size,) + message, F32),
     ] + [pltpu.VMEM(message, F32)] * 4 + [
         dma((16,)), dma((sections,)), dma((2,)), dma((2,)),
-        dma((mates,)), dma((mates,)), dma((mates,)), dma((mates,)), dma((mates,)), dma((mates,)),
+        dma((4,)), dma((4,)), dma((mates,)), dma((mates,)), dma((mates,)), dma((mates,)),
         dma((2,)), dma((2,)),
     ]
     outs = [(sections, ns), (sections, nu), (sections, ns), (sections, nu), (1, 3)]

time: 62.1 us -> 55.1 us (0.89)
  Pallas kernels: 54.6 us -> 47.6 us
    pallas_call x1, Pallas kernels: 54.6 us -> 47.6 us  [local(): pl.pallas_call(functools.partial(kernel, n, size), out_shape=[jax.ShapeDt...]
where the time goes in v2:
time: 55.1 us; the launch traced here: 54.6 us
  Pallas kernels  47.6 us (86%)
  local copies, waits for them, and re-layouts  6.35 us (12%)
  between operations  0.65 us (1%)
    pallas_call x1, Pallas kernels, local(): pl.pallas_call(functools.partial(kernel, n, size), out_shape=[jax.ShapeDt...  47.6 us
    unnamed x5, local copies, waits for them, and re-layouts  6.35 us

profile of v2, /device:TPU:24, one launch (start us, length us, event | category | flops | bytes accessed | tf_op | source)
XLA Modules:
  0.0 54.6 jit_solution(3735222342526450029)
XLA Ops:
  0.6 47.6 %shard_map.200 = (f32[16,256]{1,0:T(8,128)}, f32[16,64]{1,0:T(8,128)}, f32[16,256]{1,0:T(8,128)}, f32[16,64]{1,0:T(8,128)}, f32[1,3]{1,0:T(1,128)}) custom-call(f32[16,256,256]{2,1,0:T(8,128)} %refs_0_.1, f32[16,64,256]{2,1,0:T(8,128)} %refs_1_.1, f32[16,256,256]{2,1,0:T(8,128)} %refs_2_.1, f32[16,64,256]{2,1,0:T(8,128)} %refs_3_.1, ...), custom_call_target="tpu_custom_call" | custom-call | tf_op jit(solution)/shard_map/pallas_call | solution.py:463
  48.3 1.3 %copy.27 = f32[16,256]{1,0:T(8,128)} copy(f32[16,256]{1,0:T(8,128)} %get-tuple-element.20) | data formatting | bytes 32768
  49.6 1.3 %copy.28 = f32[16,64]{1,0:T(8,128)} copy(f32[16,64]{1,0:T(8,128)} %get-tuple-element.21) | data formatting | bytes 8192
  50.9 1.3 %copy.29 = f32[16,256]{1,0:T(8,128)} copy(f32[16,256]{1,0:T(8,128)} %get-tuple-element.22) | data formatting | bytes 32768
  52.2 1.3 %copy.30 = f32[16,64]{1,0:T(8,128)} copy(f32[16,64]{1,0:T(8,128)} %get-tuple-element.23) | data formatting | bytes 8192
  53.5 1.1 %copy.31 = f32[3]{0:T(128)} copy(f32[3]{0:T(128)} %bitcast.1) | data formatting | bytes 24
